TPU v7x, 32 devices: a whole 2x2x4 slice. The times are simulated.
32 devices in a mesh: gx: 4 (over y, x), gy: 8 (over z, core).
Axes of the slice: x: 2, y: 2, z: 4, core: 2. Of those that a mesh axis runs over, the one named last changes fastest.
Arguments:
- positions: float32 [3, 524288], P(None, ('gx', 'gy')), may hold values from -6 to 6
- normals: float32 [3, 524288], P(None, ('gx', 'gy')), may hold values from -6 to 6
- areas: float32 [524288], P(('gx', 'gy')), may hold values from 0.5 to 2
- pair_first: int32 [4096], P(('gx', 'gy')), may hold values from 0 to 2047, as said below
- pair_second: int32 [4096], P(('gx', 'gy')), may hold values from 0 to 2047, as said below
- pair_count: int32 [32], P(('gx', 'gy')), may hold values from 32 to 128, as said below
Outputs:
- gradient: float32 [3, 524288], P(None, ('gx', 'gy'))
Inputs may be any that keep to these rules, and one draw needn't show every extreme that they name: `pair_first`: slot s holds a first cluster owned by device s // 128, that is in s // 128 * 64 to (s // 128 + 1) * 64 - 1. `pair_second`: the second cluster of slot s lies on a device at most 2 away from s // 128: its index // 64 differs from s // 128 by at most 2. Dead slots hold such pairs too. `pair_count`: some device has all 128 slots live in every draw.
All inputs are finite; a program needn't handle non-finite values.
Results may differ from a plain program's by a relative error of at most 0.0001.
Values sent between devices are 32-bit elements; how exact they have to be, the bound alone decides.
No kernel may reach another device: no remote copies, remote signals or barrier semaphores. Data moves between devices by JAX's collectives and lax.ppermute only.
A program may use at most 64 MiB of HBM per device.

v0:
```python
import functools

import jax
import jax.numpy as jnp
from jax import lax
from jax.experimental import pallas as pl
from jax.experimental.pallas import tpu as pltpu
from jax.sharding import PartitionSpec as P


C = 256
AXES = ("gx", "gy")
UNROLL = 4
ROWS = 32
TABLE = 8
HEAD = 28
BALANCE = 13
F32 = jnp.float32
BF16 = jnp.bfloat16
NN = ((1,), (0,))
NT = ((1,), (1,))
TN = ((0,), (0,))


def dot(a, b, dims):
    return lax.dot_general(a, b, (dims, ((), ())), preferred_element_type=F32)


def rounded(x):
    return x.astype(BF16).astype(F32)


def two_tiles(ref, base, pitch, n):
    return jnp.concatenate([ref[pl.ds(base, n), :], ref[pl.ds(base + pitch, n), :]], axis=1)


def features(block, feat_g, g_base, feat_f, f_base):
    zero = jnp.zeros((8, 128), F32)
    one = jnp.ones((8, 128), F32)

    def step(j, carry):
        p0, p1, p2, n0, n1, n2, area = [block[pl.ds(j * 56 + k, 8, stride=7), :] for k in range(7)]
        s = jnp.exp(jnp.log(area) * (-1.0 / 3.0))
        pp = (p0 * p0 + p1 * p1 + p2 * p2 + 0.5) * s
        dot_np = n0 * p0 + n1 * p1 + n2 * p2
        q0, q1, q2 = p0 * s, p1 * s, p2 * s
        g_rows = (q0, q1, q2, pp, s, zero, zero, zero, p0, p1, p2, n0, n1, n2, dot_np, one)
        for r, v in enumerate(g_rows if feat_g is not None else ()):
            feat_g[pl.ds(g_base + j * 128 + r, 8, stride=16), :] = v
        if feat_f is not None:
            f_rows = (-2.0 * q0, -2.0 * q1, -2.0 * q2, s, pp, zero, zero, zero)
            f_rows += (-n0, -n1, -n2, zero, zero, zero, zero, dot_np)
            f_rows += (zero, zero, zero, p0, p1, p2, -one, zero)
            for r, v in enumerate(f_rows):
                feat_f[pl.ds(f_base + j * 192 + r, 8, stride=24), :] = v
        return carry

    lax.fori_loop(0, (block.shape[0] - TABLE) // 56, step, 0)


def pair_loop(lists, row, start, stop, feat_f, feat_g, acc, b_shift, dummy, scratch):
    forms, terms, weights, row_part, col_part = scratch

    def clusters(t):
        live = jnp.logical_and(t >= start, t < stop)
        safe = jnp.clip(t, start, stop - 1)
        a = lists[row, safe]
        b = lists[row + 1, safe]
        return a, b, jnp.where(live, a, dummy), jnp.where(live, b + b_shift, dummy)

    def stage(t, par):
        form_w, form_r = forms[par], forms[1 - par]
        term_w, term_r = terms[1 - par], terms[par]
        state = {}

        def prepare():
            a, b, _, _ = clusters(t)
            f = two_tiles(feat_f, pl.multiple_of(a * 48, 8), 24, 24)
            g = two_tiles(feat_g, pl.multiple_of(b * 32, 8), 16, 16)
            f1 = rounded(f)
            rest = f - f1
            f2 = rounded(rest)
            f3 = rest - f2
            g1 = rounded(g)
            rest = g - g1
            g2 = rounded(rest)
            g3 = rest - g2
            state["f"] = (f1, f2)
            state["g"] = (g1, g2)
            state["left"] = []
            for k in range(3):
                at = slice(8 * k, 8 * k + 8)
                state["left"].append(
                    jnp.concatenate([f1[at], f2[at], f3[at], f1[at], f2[at], f1[at]], axis=0)
                )
            state["right"] = []
            for k in range(2):
                at = slice(8 * k, 8 * k + 8)
                state["right"].append(
                    jnp.concatenate([g1[at], g1[at], g1[at], g2[at], g2[at], g3[at]], axis=0)
                )

        def form(k):
            def run():
                form_w[k] = dot(state["left"][k], state["right"][min(k, 1)], TN)

            return run

        def keep_weights():
            f1, f2 = state["f"]
            g1, g2 = state["g"]
            for k, (x, y) in enumerate(((f1, f2), (g1, g2))):
                for h in range(2):
                    at = slice(8 * h, 8 * h + 8)
                    rows = slice(32 * k + 16 * h, 32 * k + 16 * h + 16)
                    weights[par][rows] = jnp.concatenate([x[at], y[at]], axis=0).astype(BF16)

        col_sum = []

        def term(c):
            def run():
                rows = pl.ds(c * ROWS, ROWS)
                r2 = form_r[0, rows, :]
                sf = form_r[1, rows, :]
                sg = form_r[2, rows, :]
                inv = 1.0 / r2
                w = inv * inv * inv
                a = w * sf
                b = w * sg
                q = inv * (sf * a + sg * b)
                for m, v in enumerate((a, b, q)):
                    high = v.astype(BF16)
                    term_w[2 * m, rows, :] = high
                    term_w[2 * m + 1, rows, :] = (v - high.astype(F32)).astype(BF16)
                row_part[1 - par][rows, :] = a[:, :128] + a[:, 128:]
                part = b[0:8]
                for i in range(1, ROWS // 8):
                    part = part + b[8 * i : 8 * i + 8]
                col_sum.append(part)

            return run

        sums = {}

        def reduce(name, row, m, dims):
            def run():
                o = dot(weights[par][row : row + 16], term_r[m], dims)
                sums[name] = sums[name] + o if name in sums else o

            return run

        def plain_sums():
            turned = jnp.transpose(row_part[par][...])
            total = turned[0:8]
            for i in range(1, 16):
                total = total + turned[8 * i : 8 * i + 8]
            sums["a"] = jnp.sum(total, axis=0, keepdims=True)
            sums["b"] = jnp.sum(col_part[par][...], axis=0, keepdims=True)

        def finish():
            a, b, a_to, b_to = clusters(t - 2)

            def joined(x):
                return x[0:8] + x[8:16]

            def wide(x):
                return jnp.broadcast_to(x, (8, 256))

            col_q, col_a = joined(sums["col_q"]), joined(sums["col_a"])
            row_q, row_b = joined(sums["row_q"]), joined(sums["row_b"])
            fr = two_tiles(feat_f, pl.multiple_of(a * 48, 8), 24, 8)
            fs = two_tiles(feat_f, pl.multiple_of(a * 48 + 8, 8), 24, 8)
            gp = two_tiles(feat_g, pl.multiple_of(b * 32, 8), 16, 8)
            gq = two_tiles(feat_g, pl.multiple_of(b * 32 + 8, 8), 16, 8)
            grad_f = 3.0 * fr * wide(row_q[4:5]) + 6.0 * wide(fr[3:4]) * row_q
            grad_f = grad_f - 2.0 * fs * wide(sums["a"]) + 2.0 * pltpu.roll(row_b, 5, 0)
            grad_g = 2.0 * col_a - 2.0 * wide(sums["b"]) * pltpu.roll(gq, 5, 0)
            grad_g = grad_g - 3.0 * wide(gp[4:5]) * col_q - 6.0 * gp * wide(col_q[3:4])
            for c, g in ((a_to, grad_f), (b_to, grad_g)):
                at = pl.multiple_of(c * 16, 8)
                acc[pl.ds(at, 8), :] += g[:, :128]
                acc[pl.ds(at + 8, 8), :] += g[:, 128:]

        others = [
            prepare,
            reduce("col_a", 16, 0, NN),
            reduce("col_a", 16, 1, NN),
            form(0),
            form(1),
            form(2),
            reduce("col_q", 0, 4, NN),
            reduce("col_q", 0, 5, NN),
            reduce("row_q", 32, 4, NT),
            reduce("row_q", 32, 5, NT),
            reduce("row_b", 48, 2, NT),
            reduce("row_b", 48, 3, NT),
            plain_sums,
            finish,
            keep_weights,
        ]
        chunks = 256 // ROWS
        each = -(-len(others) // chunks)
        for c in range(chunks):
            for other in others[each * c : each * c + each]:
                other()
            term(c)()
        total = col_sum[0]
        for part in col_sum[1:]:
            total = total + part
        col_part[1 - par][...] = total

    def body(i, carry):
        for u in range(UNROLL):
            stage(start + i * UNROLL + u, u % 2)
        return carry

    trips = jnp.where(stop > start, (stop - start + 2 + UNROLL - 1) // UNROLL, 0)
    lax.fori_loop(0, trips, body, 0)


def scratch_of(rows, f_blocks, g_blocks, acc_blocks):
    return (
        [
            pltpu.VMEM((3 * f_blocks * rows, 128), F32),
            pltpu.VMEM((2 * g_blocks * rows, 128), F32),
            pltpu.VMEM((acc_blocks * rows + 16, 128), F32),
        ]
        + [pltpu.VMEM((3, 256, 256), F32)] * 2
        + [pltpu.VMEM((6, 256, 256), BF16)] * 2
        + [pltpu.VMEM((64, 256), BF16)] * 2
        + [pltpu.VMEM((256, 128), F32)] * 2
        + [pltpu.VMEM((8, 256), F32)] * 2
    )


def by_stage(scratch):
    return [scratch[2 * k : 2 * k + 2] for k in range(5)]


def compact(acc, k, r, rows):
    return acc[pl.ds(k * rows + r, rows // 8, stride=8), :]


def unpack(table, j, bits):
    code = table[j // 128, j % 128].astype(jnp.int32)
    mask = (1 << bits) - 1
    return code >> (2 * bits), code & mask, (code >> bits) & mask


def copy_table(block, table):
    pltpu.sync_copy(block.at[pl.ds(block.shape[0] - TABLE, TABLE)], table)


def append(lists, row, n, a, b, take):
    lists[row, n] = a
    lists[row + 1, n] = b
    return n + take.astype(jnp.int32)


def near_lists(odd, own, partner, lists, meta, own_table, partner_table, slots, bits):
    copy_table(own, own_table)
    copy_table(partner, partner_table)
    mine = own[pl.ds(own.shape[0] - TABLE, TABLE), :]
    its = partner[pl.ds(partner.shape[0] - TABLE, TABLE), :]
    even_codes = jnp.where(odd == 1, its, mine)
    odd_codes = jnp.where(odd == 1, mine, its)
    unit = float(1 << (2 * bits))

    def count(codes, field):
        hit = jnp.logical_and(codes >= field * unit, codes < (field + 1) * unit)
        return jnp.sum(jnp.where(hit, 1.0, 0.0)).astype(jnp.int32)

    cross_even = count(even_codes, 3)
    cross = cross_even + count(odd_codes, 1)
    odd_load = count(odd_codes, 2) + count(even_codes, 1) + count(odd_codes, 0) + BALANCE
    even_load = count(even_codes, 2) + count(even_codes, 0)
    at_even = jnp.clip((odd_load - even_load + cross) // 2, 0, cross)
    even_cut = jnp.minimum(at_even, cross_even)
    odd_cut = at_even - even_cut
    own_cut = jnp.where(odd == 1, odd_cut, even_cut)
    partner_cut = jnp.where(odd == 1, even_cut, odd_cut)
    own_cross = jnp.where(odd == 1, 1, 3)
    partner_cross = 4 - own_cross
    clusters = 1 << bits

    def step(j, carry):
        near, far, k_own, k_partner = carry
        field, f, g = unpack(own_table, j, bits)
        is_cross = field == own_cross
        mine_too = jnp.logical_xor(k_own < own_cut, odd == 1)
        take = jnp.logical_or(field == 2, jnp.logical_and(is_cross, mine_too))
        near = append(lists, 0, near, f, g + jnp.where(is_cross, clusters, 0), take)
        far = append(lists, 2, far, f, g, field == 0)
        k_own = k_own + is_cross.astype(jnp.int32)
        field, f, g = unpack(partner_table, j, bits)
        is_cross = field == partner_cross
        mine_too = jnp.logical_xor(k_partner < partner_cut, odd == 1)
        near = append(lists, 0, near, g, f + clusters, jnp.logical_and(is_cross, mine_too))
        far = append(
            lists, 2, far, f + clusters, g, jnp.logical_and(field == 1, odd == 1)
        )
        k_partner = k_partner + is_cross.astype(jnp.int32)
        return near, far, k_own, k_partner

    near, far, _, _ = lax.fori_loop(0, slots, step, (0, 0, 0, 0), unroll=4)
    meta[0] = near
    meta[1] = far
    return near


def near_kernel(slots, bits, odd, own, partner, own_out, partner_out, lists, meta, *scratch):
    own_table, partner_table, feat_f, feat_g, acc = scratch[:5]
    rows = 8 * ((own.shape[0] - TABLE) // 7)
    near = near_lists(odd[0], own, partner, lists, meta, own_table, partner_table, slots, bits)
    acc[...] = jnp.zeros_like(acc)
    features(own, feat_g, 0, feat_f, 0)
    features(partner, feat_g, 2 * rows, None, 0)
    pair_loop(
        lists, 0, 0, jnp.minimum(near, HEAD), feat_f, feat_g, acc, 0, rows // 8, by_stage(scratch[5:])
    )
    for k, out in enumerate((own_out, partner_out)):
        for r in range(3):
            out[pl.ds(r * (rows // 8), rows // 8), :] = compact(acc, k, r, rows)


def far_kernel(slots, bits, odd, meta, lists_in, own, partner, back, o0, o1, o2, *scratch):
    outs = (o0, o1, o2)
    lists, back_table, feat_f, feat_g, acc = scratch[:5]
    rows = 8 * ((own.shape[0] - TABLE) // 7)
    clusters = 1 << bits
    copy_table(back, back_table)
    known = meta[1]

    def carry_over(j, carry):
        lists[0, j] = lists_in[2, j]
        lists[1, j] = lists_in[3, j]
        return carry

    lax.fori_loop(0, known, carry_over, 0)

    def step(j, n):
        field, f, g = unpack(back_table, j, bits)
        crossed = jnp.logical_and(field == 3, odd[0] == 1)
        a = g + jnp.where(crossed, clusters, 0)
        return append(lists, 0, n, a, f, jnp.logical_or(field == 4, crossed))

    stop = lax.fori_loop(0, slots, step, known, unroll=4)
    acc[...] = jnp.zeros_like(acc)
    features(own, None, 0, feat_f, 0)
    features(back, feat_g, 0, None, 0)

    @pl.when(odd[0] == 1)
    def _():
        features(partner, None, 0, feat_f, 3 * rows)

    pair_loop(
        lists, 0, 0, stop, feat_f, feat_g, acc, 2 * (rows // 16), 3 * (rows // 16), by_stage(scratch[5:])
    )
    for k in range(3):
        for r in range(3):
            outs[k][pl.ds(r * (rows // 8), rows // 8), :] = compact(acc, k, r, rows)


def rest_kernel(
    meta, lists, own, partner, own_1, partner_1, own_2, partner_2, own_out, partner_out, *scratch
):
    feat_f, feat_g, acc = scratch[:3]
    rows = 8 * ((own.shape[0] - TABLE) // 7)
    tiles = rows // 8
    near = meta[0]

    @pl.when(near > HEAD)
    def _():
        acc[...] = jnp.zeros_like(acc)
        features(own, feat_g, 0, feat_f, 0)
        features(partner, feat_g, 2 * rows, None, 0)

    pair_loop(
        lists, 0, HEAD, near, feat_f, feat_g, acc, 0, rows // 8, by_stage(scratch[3:])
    )
    sums = ((own_out, own_1, own_2), (partner_out, partner_1, partner_2))
    for k, (out, first, second) in enumerate(sums):
        out[...] = first[...] + second[...]

        @pl.when(near > HEAD)
        def _():
            for r in range(3):
                at = pl.ds(r * tiles, tiles)
                out[at, :] += compact(acc, k, r, rows)


def call(function, ins, out_shape, scratch, smem_in, smem_out):
    smem = pl.BlockSpec(memory_space=pltpu.SMEM)
    vmem = pl.BlockSpec(memory_space=pltpu.VMEM)
    return pl.pallas_call(
        function,
        out_shape=out_shape,
        in_specs=[smem if k < smem_in else vmem for k in range(len(ins))],
        out_specs=[vmem] * (len(out_shape) - smem_out) + [smem] * smem_out,
        scratch_shapes=scratch,
        compiler_params=pltpu.CompilerParams(vmem_limit_bytes=40 * 2**20),
        cost_estimate=pl.CostEstimate(
            flops=30 * 10**9, bytes_accessed=4 * 10**6, transcendentals=0
        ),
    )(*ins)


def body(positions, normals, areas, pair_first, pair_second, pair_count):
    faces = areas.shape[0]
    clusters = faces // C
    bits = (clusters - 1).bit_length()
    tiles = faces // 128
    rows = 8 * tiles
    slots = pair_first.shape[0]
    devices = lax.axis_size(AXES)
    me = lax.axis_index(AXES)
    odd = jnp.reshape(me % 2, (1,))

    field = pair_second // clusters - me + 2
    code = (field << (2 * bits)) + ((pair_second % clusters) << bits) + pair_first % clusters
    live = jnp.arange(slots, dtype=jnp.int32) < pair_count[0]
    code = jnp.where(live, code, -1).astype(F32)
    code = jnp.pad(code, (0, TABLE * 128 - slots), constant_values=-1.0).reshape(TABLE, 128)
    geometry = jnp.concatenate([positions, normals, areas[None, :]], axis=0)
    geometry = geometry.reshape(7, tiles, 128).transpose(1, 0, 2).reshape(7 * tiles, 128)
    block = jnp.concatenate([geometry, code], axis=0)

    def permute(x, to):
        pairs = [(i, to(i)) for i in range(devices) if 0 <= to(i) < devices]
        return lax.ppermute(x, AXES, pairs)

    back = permute(block, lambda i: i + 2)
    partner = permute(block, lambda i: i ^ 1)
    part = jax.ShapeDtypeStruct((3 * tiles, 128), F32)
    lists = jax.ShapeDtypeStruct((4, 2 * slots + 8), jnp.int32)
    tables = [pltpu.SMEM((TABLE, 128), F32)]
    own_1, partner_1, lists, meta = call(
        functools.partial(near_kernel, slots, bits),
        (odd, block, partner),
        [part, part, lists, jax.ShapeDtypeStruct((2,), jnp.int32)],
        tables * 2 + scratch_of(rows, 1, 2, 2),
        1,
        2,
    )
    own_2, partner_2, back_2 = call(
        functools.partial(far_kernel, slots, bits),
        (odd, meta, lists, block, partner, back),
        [part] * 3,
        [pltpu.SMEM((2, 3 * slots + 8), jnp.int32)] + tables + scratch_of(rows, 2, 1, 3),
        3,
        0,
    )
    ahead_sum = permute(back_2, lambda i: i - 2)
    own_sum, partner_sum = call(
        rest_kernel,
        (meta, lists, block, partner, own_1, partner_1, own_2, partner_2),
        [part, part],
        scratch_of(rows, 1, 2, 2),
        2,
        0,
    )
    total = own_sum + permute(partner_sum, lambda i: i ^ 1) + ahead_sum
    return total.reshape(3, faces)


def solution(mesh):
    in_specs = (
        P(None, AXES),
        P(None, AXES),
        P(AXES),
        P(AXES),
        P(AXES),
        P(AXES),
    )
    return jax.shard_map(
        body, mesh=mesh, in_specs=in_specs, out_specs=P(None, AXES), check_vma=False
    )
```

profile of v0, /device:TPU:2, one launch (start us, length us, event | category | flops | bytes accessed | tf_op | source)
XLA Modules:
  0.0 81.7 jit_solution(1244618793718421178)
XLA Ops:
  0.7 0.0 copy-start
  0.7 0.0 copy-start.1
  0.7 0.6 copy-done
  1.3 0.0 copy-done.1
  1.4 1.2 %maximum_bitcast_fusion = f32[128,7,128]{2,1,0:T(8,128)S(1)} fusion(f32[1,128,128]{2,0,1:T(1,128)} %bitcast.12, f32[3,128,128]{2,0,1:T(4,128)} %bitcast.10, f32[3,128,128]{2,0,1:T(4,128)} %bitcast.11), kind=kLoop, calls=%fused_computation | loop fusion | flops 229376 | bytes 917504 | tf_op jit(solution)/shard_map/transpose | solution.py:425
  2.7 0.1 collective-permute-start
  2.8 3.5 %collective-permute-start.1 = (f32[904,128]{1,0:T(8,128)S(1)}, f32[904,128]{1,0:T(8,128)S(1)}, u32[]{:S(2)}, u32[]{:S(2)}) collective-permute-start(f32[904,128]{1,0:T(8,128)S(1)} %pad_maximum_fusion.own), channel_id=1, source_target_pairs={{0,2},{1,3},{2,4},{3,5},{4,6},{5,7},{6,8},{7,9},{8,10},{9,11},{10,... | collective-permute-start | bytes 1388552 | tf_op jit(solution)/shard_map/ppermute | solution.py:430
  6.3 0.0 collective-permute-done.partner
  6.3 20.0 %shard_map.64 = (f32[384,128]{1,0:T(8,128)S(1)}, f32[384,128]{1,0:T(8,128)S(1)}, s32[4,264]{1,0:T(4,128)S(1)}, s32[2]{0:T(128)S(1)}) custom-call(s32[1]{0:T(128)} %bitcast.odd, f32[904,128]{1,0:T(8,128)S(1)} %pad_maximum_fusion.own, f32[904,128]{1,0:T(8,128)S(1)} %collective-permute-done.partner), custom_call_target="tpu_custom_call" | custom-call | flops 30000001024 | bytes 4000000 | tf_op jit(solution)/shard_map/pallas_call | solution.py:395
  26.3 0.0 collective-permute-done.1.back
  26.3 24.7 %shard_map.65 = (f32[384,128]{1,0:T(8,128)S(1)}, f32[384,128]{1,0:T(8,128)S(1)}, f32[384,128]{1,0:T(8,128)S(1)}) custom-call(s32[1]{0:T(128)} %bitcast.odd, s32[2]{0:T(128)S(1)} %get-tuple-element.14.meta, s32[4,264]{1,0:T(4,128)S(1)} %get-tuple-element.15.lists_in.lists, f32[904,128]{1,0:T(8,128)S(1)} %pad_maximum_fusion.own, ...), custom_call_target="tpu_custom_call" | custom-call | flops 30000001024 | bytes 4000000 | tf_op jit(solution)/shard_map/pallas_call | solution.py:395
  51.0 20.5 %shard_map.66 = (f32[384,128]{1,0:T(8,128)S(1)}, f32[384,128]{1,0:T(8,128)S(1)}) custom-call(s32[2]{0:T(128)S(1)} %get-tuple-element.14.meta, s32[4,264]{1,0:T(4,128)S(1)} %get-tuple-element.15.lists_in.lists, f32[904,128]{1,0:T(8,128)S(1)} %pad_maximum_fusion.own, f32[904,128]{1,0:T(8,128)S(1)} %collective-permute-done.partner, ...), custom_call_target="tpu_custom_call" | custom-call | flops 30000001024 | bytes 4000000 | tf_op jit(solution)/shard_map/pallas_call | solution.py:395
  71.6 0.1 collective-permute-start.2
  71.6 1.9 %collective-permute-start.3 = (f32[384,128]{1,0:T(8,128)S(1)}, f32[384,128]{1,0:T(8,128)S(1)}, u32[]{:S(2)}, u32[]{:S(2)}) collective-permute-start(f32[384,128]{1,0:T(8,128)S(1)} %get-tuple-element.22), channel_id=1, source_target_pairs={{2,0},{3,1},{4,2},{5,3},{6,4},{7,5},{8,6},{9,7},{10,8},{11,9},{12,... | collective-permute-start | bytes 589832 | tf_op jit(solution)/shard_map/ppermute | solution.py:430
  73.6 0.0 collective-permute-done.2
  73.6 7.2 %collective-permute-done.3 = f32[384,128]{1,0:T(8,128)S(1)} collective-permute-done((f32[384,128]{1,0:T(8,128)S(1)}, f32[384,128]{1,0:T(8,128)S(1)}, u32[]{:S(2)}, u32[]{:S(2)}) %collective-permute-start.3) | collective-permute-done | bytes 196640 | tf_op jit(solution)/shard_map/ppermute | solution.py:430
  80.9 0.8 reshape.20
  (5 shorter events, 0.1 us)
Async XLA Ops:
  0.7 0.7 copy-start
  0.7 0.7 copy-start.1
  2.7 3.6 %collective-permute-start = (f32[904,128]{1,0:T(8,128)S(1)}, f32[904,128]{1,0:T(8,128)S(1)}, u32[]{:S(2)}, u32[]{:S(2)}) collective-permute-start(f32[904,128]{1,0:T(8,128)S(1)} %pad_maximum_fusion.own), channel_id=1, source_target_pairs={{0,1},{1,0},{2,3},{3,2},{4,5},{5,4},{6,7},{7,6},{8,9},{9,8},{10,11... | collective-permute-start | bytes 1388552 | tf_op jit(solution)/shard_map/ppermute | solution.py:430
  2.8 23.5 %collective-permute-start.1 = (f32[904,128]{1,0:T(8,128)S(1)}, f32[904,128]{1,0:T(8,128)S(1)}, u32[]{:S(2)}, u32[]{:S(2)}) collective-permute-start(f32[904,128]{1,0:T(8,128)S(1)} %pad_maximum_fusion.own), channel_id=1, source_target_pairs={{0,2},{1,3},{2,4},{3,5},{4,6},{5,7},{6,8},{7,9},{8,10},{9,11},{10,... | collective-permute-start | bytes 1388552 | tf_op jit(solution)/shard_map/ppermute | solution.py:430
  71.6 2.0 %collective-permute-start.2 = (f32[384,128]{1,0:T(8,128)S(1)}, f32[384,128]{1,0:T(8,128)S(1)}, u32[]{:S(2)}, u32[]{:S(2)}) collective-permute-start(f32[384,128]{1,0:T(8,128)S(1)} %get-tuple-element.21), channel_id=1, source_target_pairs={{0,1},{1,0},{2,3},{3,2},{4,5},{5,4},{6,7},{7,6},{8,9},{9,8},{10,11... | collective-permute-start | bytes 589832 | tf_op jit(solution)/shard_map/ppermute | solution.py:430
  71.6 9.2 %collective-permute-start.3 = (f32[384,128]{1,0:T(8,128)S(1)}, f32[384,128]{1,0:T(8,128)S(1)}, u32[]{:S(2)}, u32[]{:S(2)}) collective-permute-start(f32[384,128]{1,0:T(8,128)S(1)} %get-tuple-element.22), channel_id=1, source_target_pairs={{2,0},{3,1},{4,2},{5,3},{6,4},{7,5},{8,6},{9,7},{10,8},{11,9},{12,... | collective-permute-start | bytes 589832 | tf_op jit(solution)/shard_map/ppermute | solution.py:430
where the time goes:
time: 81.8 us; the launch traced here: 81.7 us
  Pallas kernels  65.2 us (80%)
  waiting for transfers between devices  7.25 us (9%)
  starting transfers between devices  5.55 us (7%)
  local copies, waits for them, and re-layouts  1.51 us (2%)
  other arithmetic  1.32 us (2%)
    pallas_call x3, Pallas kernels, call(): pl.pallas_call(function, out_shape=out_shape, in_specs=[smem if k < smem_...  65.2 us
    ppermute x4, waiting for transfers between devices, permute(): return lax.ppermute(x, AXES, pairs)  7.25 us
    ppermute x4, starting transfers between devices, permute(): return lax.ppermute(x, AXES, pairs)  5.55 us
  transfers between devices with their start and end apart: 4, of which 1 were waited for; matrix products, arithmetic and copies ran while one was open for 0% of the time, Pallas kernels for 24%

commit v1 on v0

--- a/solution.py
+++ b/solution.py
@@ -58,14 +58,13 @@
     lax.fori_loop(0, (block.shape[0] - TABLE) // 56, step, 0)
 
 
-def pair_loop(lists, row, start, stop, feat_f, feat_g, acc, b_shift, dummy, scratch):
+def pair_loop(lookup, start, stop, feat_f, feat_g, acc, b_shift, dummy, scratch):
     forms, terms, weights, row_part, col_part = scratch
 
     def clusters(t):
         live = jnp.logical_and(t >= start, t < stop)
         safe = jnp.clip(t, start, stop - 1)
-        a = lists[row, safe]
-        b = lists[row + 1, safe]
+        a, b = lookup(safe)
         return a, b, jnp.where(live, a, dummy), jnp.where(live, b + b_shift, dummy)
 
     def stage(t, par):
@@ -182,18 +181,18 @@
                 acc[pl.ds(at + 8, 8), :] += g[:, 128:]
 
         others = [
-            prepare,
-            reduce("col_a", 16, 0, NN),
-            reduce("col_a", 16, 1, NN),
-            form(0),
-            form(1),
-            form(2),
-            reduce("col_q", 0, 4, NN),
-            reduce("col_q", 0, 5, NN),
             reduce("row_q", 32, 4, NT),
             reduce("row_q", 32, 5, NT),
             reduce("row_b", 48, 2, NT),
             reduce("row_b", 48, 3, NT),
+            reduce("col_a", 16, 0, NN),
+            reduce("col_a", 16, 1, NN),
+            reduce("col_q", 0, 4, NN),
+            reduce("col_q", 0, 5, NN),
+            prepare,
+            form(0),
+            form(1),
+            form(2),
             plain_sums,
             finish,
             keep_weights,
@@ -218,13 +217,9 @@
     lax.fori_loop(0, trips, body, 0)
 
 
-def scratch_of(rows, f_blocks, g_blocks, acc_blocks):
+def scratch_of(rows, acc_blocks):
     return (
-        [
-            pltpu.VMEM((3 * f_blocks * rows, 128), F32),
-            pltpu.VMEM((2 * g_blocks * rows, 128), F32),
-            pltpu.VMEM((acc_blocks * rows + 16, 128), F32),
-        ]
+        [pltpu.VMEM((acc_blocks * rows + 16, 128), F32)]
         + [pltpu.VMEM((3, 256, 256), F32)] * 2
         + [pltpu.VMEM((6, 256, 256), BF16)] * 2
         + [pltpu.VMEM((64, 256), BF16)] * 2
@@ -241,162 +236,181 @@
     return acc[pl.ds(k * rows + r, rows // 8, stride=8), :]
 
 
-def unpack(table, j, bits):
-    code = table[j // 128, j % 128].astype(jnp.int32)
+def sort_kernel(unit, code_ref, out):
+    code = code_ref[...]
+    slots = code.shape[1]
+    shape = (slots, slots)
+    column = jnp.transpose(jnp.broadcast_to(code, (8, slots)))[:, 0:1]
+    lane = lax.broadcasted_iota(jnp.int32, shape, 1).astype(F32)
+    sublane = lax.broadcasted_iota(jnp.int32, shape, 0).astype(F32)
+    field_row = jnp.floor(jnp.broadcast_to(code, shape) * (1.0 / unit))
+    field_column = jnp.floor(jnp.broadcast_to(column, shape) * (1.0 / unit))
+    before = field_row * slots + lane < field_column * slots + sublane
+    rank = jnp.sum(jnp.where(before, 1.0, 0.0), axis=1, keepdims=True)
+    ordered = jnp.sum(jnp.where(rank == lane, column, 0.0), axis=0, keepdims=True)
+    starts = jnp.sum(jnp.where(field_column < lane, 1.0, 0.0), axis=0, keepdims=True)
+    out[...] = jnp.zeros_like(out)
+    for r in range(slots // 128):
+        out[r : r + 1, :] = ordered[:, 128 * r : 128 * r + 128]
+    out[slots // 128 : slots // 128 + 1, :] = starts[:, :128]
+
+
+def table_copies(blocks, table, sems):
+    copies = []
+    for k, block in enumerate(blocks):
+        part = block.at[pl.ds(block.shape[0] - TABLE, TABLE)]
+        copies.append(
+            pltpu.make_async_copy(part, table.at[pl.ds(k * TABLE, TABLE)], sems.at[k])
+        )
+    for copy in copies:
+        copy.start()
+    return copies
+
+
+def starts_of(table, k, slots):
+    row = k * TABLE + slots // 128
+    return [table[row, i].astype(jnp.int32) for i in range(6)]
+
+
+def planner(table, bits, segments):
     mask = (1 << bits) - 1
-    return code >> (2 * bits), code & mask, (code >> bits) & mask
-
-
-def copy_table(block, table):
-    pltpu.sync_copy(block.at[pl.ds(block.shape[0] - TABLE, TABLE)], table)
-
-
-def append(lists, row, n, a, b, take):
-    lists[row, n] = a
-    lists[row + 1, n] = b
-    return n + take.astype(jnp.int32)
-
-
-def near_lists(odd, own, partner, lists, meta, own_table, partner_table, slots, bits):
-    copy_table(own, own_table)
-    copy_table(partner, partner_table)
-    mine = own[pl.ds(own.shape[0] - TABLE, TABLE), :]
-    its = partner[pl.ds(partner.shape[0] - TABLE, TABLE), :]
-    even_codes = jnp.where(odd == 1, its, mine)
-    odd_codes = jnp.where(odd == 1, mine, its)
-    unit = float(1 << (2 * bits))
-
-    def count(codes, field):
-        hit = jnp.logical_and(codes >= field * unit, codes < (field + 1) * unit)
-        return jnp.sum(jnp.where(hit, 1.0, 0.0)).astype(jnp.int32)
-
-    cross_even = count(even_codes, 3)
-    cross = cross_even + count(odd_codes, 1)
-    odd_load = count(odd_codes, 2) + count(even_codes, 1) + count(odd_codes, 0) + BALANCE
-    even_load = count(even_codes, 2) + count(even_codes, 0)
+    ends = []
+    total = 0
+    for length, *_ in segments:
+        total = total + length
+        ends.append(total)
+
+    def lookup(t):
+        _, base, swapped, a_add, b_add = segments[0]
+        shift = base
+        for k in range(1, len(segments)):
+            _, base, swap_k, a_k, b_k = segments[k]
+            past = t >= ends[k - 1]
+            shift = jnp.where(past, base - ends[k - 1], shift)
+            swapped = jnp.where(past, swap_k, swapped)
+            a_add = jnp.where(past, a_k, a_add)
+            b_add = jnp.where(past, b_k, b_add)
+        at = t + shift
+        code = table[at >> 7, at & 127].astype(jnp.int32)
+        f = code & mask
+        g = (code >> bits) & mask
+        return jnp.where(swapped == 1, g, f) + a_add, jnp.where(swapped == 1, f, g) + b_add
+
+    return lookup, total
+
+
+def near_plan(odd, table, slots, bits):
+    mine = starts_of(table, 0, slots)
+    its = starts_of(table, 1, slots)
+    even = [jnp.where(odd == 1, y, x) for x, y in zip(mine, its)]
+    odds = [jnp.where(odd == 1, x, y) for x, y in zip(mine, its)]
+
+    def count(starts, field):
+        return starts[field + 1] - starts[field]
+
+    cross_even = count(even, 3)
+    cross_odd = count(odds, 1)
+    cross = cross_even + cross_odd
+    odd_load = count(odds, 2) + count(even, 1) + count(odds, 0) + BALANCE
+    even_load = count(even, 2) + count(even, 0)
     at_even = jnp.clip((odd_load - even_load + cross) // 2, 0, cross)
     even_cut = jnp.minimum(at_even, cross_even)
     odd_cut = at_even - even_cut
-    own_cut = jnp.where(odd == 1, odd_cut, even_cut)
-    partner_cut = jnp.where(odd == 1, even_cut, odd_cut)
-    own_cross = jnp.where(odd == 1, 1, 3)
-    partner_cross = 4 - own_cross
+    far_table = TABLE * 128
     clusters = 1 << bits
-
-    def step(j, carry):
-        near, far, k_own, k_partner = carry
-        field, f, g = unpack(own_table, j, bits)
-        is_cross = field == own_cross
-        mine_too = jnp.logical_xor(k_own < own_cut, odd == 1)
-        take = jnp.logical_or(field == 2, jnp.logical_and(is_cross, mine_too))
-        near = append(lists, 0, near, f, g + jnp.where(is_cross, clusters, 0), take)
-        far = append(lists, 2, far, f, g, field == 0)
-        k_own = k_own + is_cross.astype(jnp.int32)
-        field, f, g = unpack(partner_table, j, bits)
-        is_cross = field == partner_cross
-        mine_too = jnp.logical_xor(k_partner < partner_cut, odd == 1)
-        near = append(lists, 0, near, g, f + clusters, jnp.logical_and(is_cross, mine_too))
-        far = append(
-            lists, 2, far, f + clusters, g, jnp.logical_and(field == 1, odd == 1)
-        )
-        k_partner = k_partner + is_cross.astype(jnp.int32)
-        return near, far, k_own, k_partner
-
-    near, far, _, _ = lax.fori_loop(0, slots, step, (0, 0, 0, 0), unroll=4)
-    meta[0] = near
-    meta[1] = far
-    return near
-
-
-def near_kernel(slots, bits, odd, own, partner, own_out, partner_out, lists, meta, *scratch):
-    own_table, partner_table, feat_f, feat_g, acc = scratch[:5]
+    own_at = jnp.where(odd == 1, mine[1] + odd_cut, mine[3])
+    own_len = jnp.where(odd == 1, cross_odd - odd_cut, even_cut)
+    its_at = jnp.where(odd == 1, its[3] + even_cut, its[1])
+    its_len = jnp.where(odd == 1, cross_even - even_cut, odd_cut)
+    return planner(
+        table,
+        bits,
+        [
+            (count(mine, 2), mine[2], 0, 0, 0),
+            (own_len, own_at, 0, 0, clusters),
+            (its_len, its_at + far_table, 1, 0, clusters),
+        ],
+    )
+
+
+def near_kernel(slots, bits, odd, own, partner, own_out, partner_out, feat_f, feat_g, *scratch):
+    table, sems, acc = scratch[:3]
     rows = 8 * ((own.shape[0] - TABLE) // 7)
-    near = near_lists(odd[0], own, partner, lists, meta, own_table, partner_table, slots, bits)
+    copies = table_copies((own, partner), table, sems)
+    features(own, feat_g, 0, feat_f, 0)
+    features(partner, feat_g, 2 * rows, feat_f, 3 * rows)
     acc[...] = jnp.zeros_like(acc)
-    features(own, feat_g, 0, feat_f, 0)
-    features(partner, feat_g, 2 * rows, None, 0)
-    pair_loop(
-        lists, 0, 0, jnp.minimum(near, HEAD), feat_f, feat_g, acc, 0, rows // 8, by_stage(scratch[5:])
-    )
+    for copy in copies:
+        copy.wait()
+    lookup, near = near_plan(odd[0], table, slots, bits)
+    stop = jnp.minimum(near, HEAD)
+    pair_loop(lookup, 0, stop, feat_f, feat_g, acc, 0, rows // 8, by_stage(scratch[3:]))
     for k, out in enumerate((own_out, partner_out)):
         for r in range(3):
             out[pl.ds(r * (rows // 8), rows // 8), :] = compact(acc, k, r, rows)
 
 
-def far_kernel(slots, bits, odd, meta, lists_in, own, partner, back, o0, o1, o2, *scratch):
-    outs = (o0, o1, o2)
-    lists, back_table, feat_f, feat_g, acc = scratch[:5]
+def far_kernel(slots, bits, odd_ref, own, partner, back, feat_f, o0, o1, o2, *scratch):
+    table, sems, feat_g, acc = scratch[:4]
     rows = 8 * ((own.shape[0] - TABLE) // 7)
+    copies = table_copies((own, partner, back), table, sems)
+    features(back, feat_g, 0, None, 0)
+    acc[...] = jnp.zeros_like(acc)
+    for copy in copies:
+        copy.wait()
+    odd = odd_ref[0]
+    mine, its, theirs = [starts_of(table, k, slots) for k in range(3)]
+    unit = TABLE * 128
     clusters = 1 << bits
-    copy_table(back, back_table)
-    known = meta[1]
-
-    def carry_over(j, carry):
-        lists[0, j] = lists_in[2, j]
-        lists[1, j] = lists_in[3, j]
-        return carry
-
-    lax.fori_loop(0, known, carry_over, 0)
-
-    def step(j, n):
-        field, f, g = unpack(back_table, j, bits)
-        crossed = jnp.logical_and(field == 3, odd[0] == 1)
-        a = g + jnp.where(crossed, clusters, 0)
-        return append(lists, 0, n, a, f, jnp.logical_or(field == 4, crossed))
-
-    stop = lax.fori_loop(0, slots, step, known, unroll=4)
-    acc[...] = jnp.zeros_like(acc)
-    features(own, None, 0, feat_f, 0)
-    features(back, feat_g, 0, None, 0)
-
-    @pl.when(odd[0] == 1)
-    def _():
-        features(partner, None, 0, feat_f, 3 * rows)
-
+    lookup, far = planner(
+        table,
+        bits,
+        [
+            (mine[1], 0, 0, 0, 0),
+            (odd * (its[2] - its[1]), its[1] + unit, 0, clusters, 0),
+            (theirs[5] - theirs[4], theirs[4] + 2 * unit, 1, 0, 0),
+            (odd * (theirs[4] - theirs[3]), theirs[3] + 2 * unit, 1, clusters, 0),
+        ],
+    )
     pair_loop(
-        lists, 0, 0, stop, feat_f, feat_g, acc, 2 * (rows // 16), 3 * (rows // 16), by_stage(scratch[5:])
-    )
-    for k in range(3):
+        lookup, 0, far, feat_f, feat_g, acc, rows // 8, 3 * (rows // 16), by_stage(scratch[4:])
+    )
+    for k, out in enumerate((o0, o1, o2)):
         for r in range(3):
-            outs[k][pl.ds(r * (rows // 8), rows // 8), :] = compact(acc, k, r, rows)
+            out[pl.ds(r * (rows // 8), rows // 8), :] = compact(acc, k, r, rows)
 
 
 def rest_kernel(
-    meta, lists, own, partner, own_1, partner_1, own_2, partner_2, own_out, partner_out, *scratch
+    slots, bits, odd, own, partner, feat_f, feat_g, own_1, partner_1, own_2, partner_2, own_out, partner_out, *scratch
 ):
-    feat_f, feat_g, acc = scratch[:3]
+    table, sems, acc = scratch[:3]
     rows = 8 * ((own.shape[0] - TABLE) // 7)
     tiles = rows // 8
-    near = meta[0]
+    copies = table_copies((own, partner), table, sems)
+    sums = ((own_out, own_1, own_2), (partner_out, partner_1, partner_2))
+    for out, first, second in sums:
+        out[...] = first[...] + second[...]
+    for copy in copies:
+        copy.wait()
+    lookup, near = near_plan(odd[0], table, slots, bits)
 
     @pl.when(near > HEAD)
     def _():
         acc[...] = jnp.zeros_like(acc)
-        features(own, feat_g, 0, feat_f, 0)
-        features(partner, feat_g, 2 * rows, None, 0)
-
-    pair_loop(
-        lists, 0, HEAD, near, feat_f, feat_g, acc, 0, rows // 8, by_stage(scratch[3:])
-    )
-    sums = ((own_out, own_1, own_2), (partner_out, partner_1, partner_2))
-    for k, (out, first, second) in enumerate(sums):
-        out[...] = first[...] + second[...]
-
-        @pl.when(near > HEAD)
-        def _():
+        pair_loop(lookup, HEAD, near, feat_f, feat_g, acc, 0, rows // 8, by_stage(scratch[3:]))
+        for k, (out, _, _) in enumerate(sums):
             for r in range(3):
-                at = pl.ds(r * tiles, tiles)
-                out[at, :] += compact(acc, k, r, rows)
-
-
-def call(function, ins, out_shape, scratch, smem_in, smem_out):
+                out[pl.ds(r * tiles, tiles), :] += compact(acc, k, r, rows)
+
+
+def call(function, ins, out_shape, scratch, smem_in=1):
     smem = pl.BlockSpec(memory_space=pltpu.SMEM)
     vmem = pl.BlockSpec(memory_space=pltpu.VMEM)
     return pl.pallas_call(
         function,
         out_shape=out_shape,
         in_specs=[smem if k < smem_in else vmem for k in range(len(ins))],
-        out_specs=[vmem] * (len(out_shape) - smem_out) + [smem] * smem_out,
+        out_specs=[vmem] * len(out_shape),
         scratch_shapes=scratch,
         compiler_params=pltpu.CompilerParams(vmem_limit_bytes=40 * 2**20),
         cost_estimate=pl.CostEstimate(
@@ -418,12 +432,19 @@
 
     field = pair_second // clusters - me + 2
     code = (field << (2 * bits)) + ((pair_second % clusters) << bits) + pair_first % clusters
+    unit = float(1 << (2 * bits))
     live = jnp.arange(slots, dtype=jnp.int32) < pair_count[0]
-    code = jnp.where(live, code, -1).astype(F32)
-    code = jnp.pad(code, (0, TABLE * 128 - slots), constant_values=-1.0).reshape(TABLE, 128)
+    code = jnp.where(live, code.astype(F32), 5.0 * unit).reshape(1, slots)
+    (table,) = call(
+        functools.partial(sort_kernel, unit),
+        (code,),
+        [jax.ShapeDtypeStruct((TABLE, 128), F32)],
+        [],
+        0,
+    )
     geometry = jnp.concatenate([positions, normals, areas[None, :]], axis=0)
     geometry = geometry.reshape(7, tiles, 128).transpose(1, 0, 2).reshape(7 * tiles, 128)
-    block = jnp.concatenate([geometry, code], axis=0)
+    block = jnp.concatenate([geometry, table], axis=0)
 
     def permute(x, to):
         pairs = [(i, to(i)) for i in range(devices) if 0 <= to(i) < devices]
@@ -432,32 +453,30 @@
     back = permute(block, lambda i: i + 2)
     partner = permute(block, lambda i: i ^ 1)
     part = jax.ShapeDtypeStruct((3 * tiles, 128), F32)
-    lists = jax.ShapeDtypeStruct((4, 2 * slots + 8), jnp.int32)
-    tables = [pltpu.SMEM((TABLE, 128), F32)]
-    own_1, partner_1, lists, meta = call(
+    f_rows = jax.ShapeDtypeStruct((6 * rows, 128), F32)
+    g_rows = jax.ShapeDtypeStruct((4 * rows, 128), F32)
+
+    def tables(count):
+        return [pltpu.SMEM((count * TABLE, 128), F32), pltpu.SemaphoreType.DMA((count,))]
+
+    own_1, partner_1, feat_f, feat_g = call(
         functools.partial(near_kernel, slots, bits),
         (odd, block, partner),
-        [part, part, lists, jax.ShapeDtypeStruct((2,), jnp.int32)],
-        tables * 2 + scratch_of(rows, 1, 2, 2),
-        1,
-        2,
+        [part, part, f_rows, g_rows],
+        tables(2) + scratch_of(rows, 2),
     )
     own_2, partner_2, back_2 = call(
         functools.partial(far_kernel, slots, bits),
-        (odd, meta, lists, block, partner, back),
+        (odd, block, partner, back, feat_f),
         [part] * 3,
-        [pltpu.SMEM((2, 3 * slots + 8), jnp.int32)] + tables + scratch_of(rows, 2, 1, 3),
-        3,
-        0,
+        tables(3) + [pltpu.VMEM((2 * rows, 128), F32)] + scratch_of(rows, 3),
     )
     ahead_sum = permute(back_2, lambda i: i - 2)
     own_sum, partner_sum = call(
-        rest_kernel,
-        (meta, lists, block, partner, own_1, partner_1, own_2, partner_2),
+        functools.partial(rest_kernel, slots, bits),
+        (odd, block, partner, feat_f, feat_g, own_1, partner_1, own_2, partner_2),
         [part, part],
-        scratch_of(rows, 1, 2, 2),
-        2,
-        0,
+        tables(2) + scratch_of(rows, 2),
     )
     total = own_sum + permute(partner_sum, lambda i: i ^ 1) + ahead_sum
     return total.reshape(3, faces)

time: 81.8 us -> 66.6 us (0.81)
  Pallas kernels: 65.2 us -> 48.8 us
  waiting for transfers between devices: 7.25 us -> 8.82 us
    pallas_call x3 -> x4, Pallas kernels: 65.2 us -> 48.8 us  [call(): pl.pallas_call(function, out_shape=out_shape, in_specs=[smem if k < smem_...]
    ppermute x4, waiting for transfers between devices: 7.25 us -> 8.82 us  [permute(): return lax.ppermute(x, AXES, pairs)]
    transpose x1, other arithmetic: 1.24 us -> 0.17 us  [body(): geometry.reshape(7, tiles, 128).transpose(1, 0, 2).reshape(7 * tiles, 128)]
  transfers between devices with their start and end apart: 4 -> 4, of which waited for: 1 -> 2; matrix products, arithmetic and copies ran while one was open for 0% -> 0% of each run, Pallas kernels for 24% -> 19%
where the time goes in v1:
time: 66.6 us; the launch traced here: 66.4 us
  Pallas kernels  48.8 us (73%)
  waiting for transfers between devices  8.82 us (13%)
  starting transfers between devices  5.55 us (8%)
  local copies, waits for them, and re-layouts  1.6 us (2%)
  other arithmetic  0.93 us (1%)
  between operations  0.79 us (1%)
    pallas_call x4, Pallas kernels, call(): pl.pallas_call(function, out_shape=out_shape, in_specs=[smem if k < smem_...  48.8 us
    ppermute x4, waiting for transfers between devices, permute(): return lax.ppermute(x, AXES, pairs)  8.82 us
    ppermute x4, starting transfers between devices, permute(): return lax.ppermute(x, AXES, pairs)  5.55 us
  transfers between devices with their start and end apart: 4, of which 2 were waited for; matrix products, arithmetic and copies ran while one was open for 0% of the time, Pallas kernels for 19%

profile of v1, /device:TPU:2, one launch (start us, length us, event | category | flops | bytes accessed | tf_op | source)
XLA Modules:
  0.0 66.4 jit_solution(9410868681739995946)
XLA Ops:
  0.7 0.7 %fusion.1.code_ref = f32[1,128]{1,0:T(1,128)S(1)} fusion(s32[128]{0:T(128)} %param.9, s32[128]{0:T(128)} %param.10, s32[]{:T(128)S(6)} %add.36, s32[]{:T(128)} %bitcast.9), kind=kLoop, calls=%fused_computation.13 | loop fusion | flops 4992 | bytes 1544 | tf_op jit(solution)/shard_map/reshape | solution.py:437
  1.3 0.0 copy-start
  1.4 0.0 copy-start.1
  1.4 0.0 copy-start.2
  1.4 0.3 shard_map.64
  1.6 0.7 copy-done
  2.3 0.1 copy-done.1
  2.4 0.0 copy-done.2
  2.4 0.2 maximum_bitcast_fusion
  2.7 0.1 collective-permute-start
  2.7 3.5 %collective-permute-start.1 = (f32[904,128]{1,0:T(8,128)S(1)}, f32[904,128]{1,0:T(8,128)S(1)}, u32[]{:S(2)}, u32[]{:S(2)}) collective-permute-start(f32[904,128]{1,0:T(8,128)S(1)} %pad_maximum_fusion.own), channel_id=1, source_target_pairs={{0,2},{1,3},{2,4},{3,5},{4,6},{5,7},{6,8},{7,9},{8,10},{9,11},{10,... | collective-permute-start | bytes 1388552 | tf_op jit(solution)/shard_map/ppermute | solution.py:451
  6.2 0.0 collective-permute-done.partner
  6.2 12.5 %shard_map.65 = (f32[384,128]{1,0:T(8,128)S(1)}, f32[384,128]{1,0:T(8,128)S(1)}, f32[6144,128]{1,0:T(8,128)S(1)}, f32[4096,128]{1,0:T(8,128)S(1)}) custom-call(s32[1]{0:T(128)} %bitcast.odd.odd_ref, f32[904,128]{1,0:T(8,128)S(1)} %pad_maximum_fusion.own, f32[904,128]{1,0:T(8,128)S(1)} %collective-permute-done.partner), custom_call_target="tpu_custom_call" | custom-call | flops 30000001024 | bytes 4000000 | tf_op jit(solution)/shard_map/pallas_call | solution.py:409
  18.8 1.6 %collective-permute-done.1.back = f32[904,128]{1,0:T(8,128)S(1)} collective-permute-done((f32[904,128]{1,0:T(8,128)S(1)}, f32[904,128]{1,0:T(8,128)S(1)}, u32[]{:S(2)}, u32[]{:S(2)}) %collective-permute-start.1) | collective-permute-done | bytes 462880 | tf_op jit(solution)/shard_map/ppermute | solution.py:451
  20.3 18.6 %shard_map.66 = (f32[384,128]{1,0:T(8,128)S(1)}, f32[384,128]{1,0:T(8,128)S(1)}, f32[384,128]{1,0:T(8,128)S(1)}) custom-call(s32[1]{0:T(128)} %bitcast.odd.odd_ref, f32[904,128]{1,0:T(8,128)S(1)} %pad_maximum_fusion.own, f32[904,128]{1,0:T(8,128)S(1)} %collective-permute-done.partner, f32[904,128]{1,0:T(8,128)S(1)} %collective-permute-done.1.back, ...), custom_call_target="tpu_custom_call" | custom-call | flops 30000001024 | bytes 4000000 | tf_op jit(solution)/shard_map/pallas_call | solution.py:409
  39.0 17.3 %shard_map.67 = (f32[384,128]{1,0:T(8,128)S(1)}, f32[384,128]{1,0:T(8,128)S(1)}) custom-call(s32[1]{0:T(128)} %bitcast.odd.odd_ref, f32[904,128]{1,0:T(8,128)S(1)} %pad_maximum_fusion.own, f32[904,128]{1,0:T(8,128)S(1)} %collective-permute-done.partner, f32[6144,128]{1,0:T(8,128)S(1)} %get-tuple-element.14.feat_f, f32[4096,128]{1,0:T(8,128)S(1)} %get-tuple-element.15.feat_g, ...), custom_call_target="tpu_custom_call" | custom-call | flops 30000001024 | bytes 4000000 | tf_op jit(solution)/shard_map/pallas_call | solution.py:409
  56.3 0.1 collective-permute-start.2
  56.4 1.9 %collective-permute-start.3 = (f32[384,128]{1,0:T(8,128)S(1)}, f32[384,128]{1,0:T(8,128)S(1)}, u32[]{:S(2)}, u32[]{:S(2)}) collective-permute-start(f32[384,128]{1,0:T(8,128)S(1)} %get-tuple-element.22), channel_id=1, source_target_pairs={{2,0},{3,1},{4,2},{5,3},{6,4},{7,5},{8,6},{9,7},{10,8},{11,9},{12,... | collective-permute-start | bytes 589832 | tf_op jit(solution)/shard_map/ppermute | solution.py:451
  58.3 0.0 collective-permute-done.2
  58.3 7.2 %collective-permute-done.3 = f32[384,128]{1,0:T(8,128)S(1)} collective-permute-done((f32[384,128]{1,0:T(8,128)S(1)}, f32[384,128]{1,0:T(8,128)S(1)}, u32[]{:S(2)}, u32[]{:S(2)}) %collective-permute-start.3) | collective-permute-done | bytes 196640 | tf_op jit(solution)/shard_map/ppermute | solution.py:451
  65.6 0.8 %reshape.20 = f32[3,16384]{1,0:T(4,128)} reshape(f32[384,128]{1,0:T(8,128)S(1)} %add_add_fusion) | data formatting | bytes 393216 | tf_op jit(solution)/shard_map/reshape | solution.py:482
  (3 shorter events, 0.1 us)
Async XLA Ops:
  1.3 1.0 %copy-start = (f32[3,16384]{1,0:T(4,128)S(1)}, f32[3,16384]{1,0:T(4,128)}, u32[]{:S(2)}) copy-start(f32[3,16384]{1,0:T(4,128)} %param.7) | copy-start | bytes 589828
  1.4 1.0 %copy-start.1 = (f32[3,16384]{1,0:T(4,128)S(1)}, f32[3,16384]{1,0:T(4,128)}, u32[]{:S(2)}) copy-start(f32[3,16384]{1,0:T(4,128)} %param.6) | copy-start | bytes 589828
  1.4 1.0 %copy-start.2 = (f32[16384]{0:T(1024)S(1)}, f32[16384]{0:T(1024)}, u32[]{:S(2)}) copy-start(f32[16384]{0:T(1024)} %param.8) | copy-start | bytes 196612
  2.7 3.6 %collective-permute-start = (f32[904,128]{1,0:T(8,128)S(1)}, f32[904,128]{1,0:T(8,128)S(1)}, u32[]{:S(2)}, u32[]{:S(2)}) collective-permute-start(f32[904,128]{1,0:T(8,128)S(1)} %pad_maximum_fusion.own), channel_id=1, source_target_pairs={{0,1},{1,0},{2,3},{3,2},{4,5},{5,4},{6,7},{7,6},{8,9},{9,8},{10,11... | collective-permute-start | bytes 1388552 | tf_op jit(solution)/shard_map/ppermute | solution.py:451
  2.7 17.6 %collective-permute-start.1 = (f32[904,128]{1,0:T(8,128)S(1)}, f32[904,128]{1,0:T(8,128)S(1)}, u32[]{:S(2)}, u32[]{:S(2)}) collective-permute-start(f32[904,128]{1,0:T(8,128)S(1)} %pad_maximum_fusion.own), channel_id=1, source_target_pairs={{0,2},{1,3},{2,4},{3,5},{4,6},{5,7},{6,8},{7,9},{8,10},{9,11},{10,... | collective-permute-start | bytes 1388552 | tf_op jit(solution)/shard_map/ppermute | solution.py:451
  56.3 2.0 %collective-permute-start.2 = (f32[384,128]{1,0:T(8,128)S(1)}, f32[384,128]{1,0:T(8,128)S(1)}, u32[]{:S(2)}, u32[]{:S(2)}) collective-permute-start(f32[384,128]{1,0:T(8,128)S(1)} %get-tuple-element.21), channel_id=1, source_target_pairs={{0,1},{1,0},{2,3},{3,2},{4,5},{5,4},{6,7},{7,6},{8,9},{9,8},{10,11... | collective-permute-start | bytes 589832 | tf_op jit(solution)/shard_map/ppermute | solution.py:451
  56.4 9.2 %collective-permute-start.3 = (f32[384,128]{1,0:T(8,128)S(1)}, f32[384,128]{1,0:T(8,128)S(1)}, u32[]{:S(2)}, u32[]{:S(2)}) collective-permute-start(f32[384,128]{1,0:T(8,128)S(1)} %get-tuple-element.22), channel_id=1, source_target_pairs={{2,0},{3,1},{4,2},{5,3},{6,4},{7,5},{8,6},{9,7},{10,8},{11,9},{12,... | collective-permute-start | bytes 589832 | tf_op jit(solution)/shard_map/ppermute | solution.py:451

commit v2 on v1

--- a/solution.py
+++ b/solution.py
@@ -11,6 +11,7 @@
 C = 256
 AXES = ("gx", "gy")
 UNROLL = 4
+FAR_UNROLL = 12
 ROWS = 32
 TABLE = 8
 HEAD = 28
@@ -58,7 +59,7 @@
     lax.fori_loop(0, (block.shape[0] - TABLE) // 56, step, 0)
 
 
-def pair_loop(lookup, start, stop, feat_f, feat_g, acc, b_shift, dummy, scratch):
+def pair_loop(lookup, start, stop, feat_f, feat_g, acc, b_shift, dummy, scratch, unroll=UNROLL):
     forms, terms, weights, row_part, col_part = scratch
 
     def clusters(t):
@@ -208,13 +209,22 @@
             total = total + part
         col_part[1 - par][...] = total
 
-    def body(i, carry):
-        for u in range(UNROLL):
-            stage(start + i * UNROLL + u, u % 2)
-        return carry
-
-    trips = jnp.where(stop > start, (stop - start + 2 + UNROLL - 1) // UNROLL, 0)
-    lax.fori_loop(0, trips, body, 0)
+    def stages(at, step):
+        def body(i, carry):
+            for u in range(step):
+                stage(at + i * step + u, u % 2)
+            return carry
+
+        return body
+
+    needed = jnp.where(stop > start, stop - start + 2, 0)
+    done = 0
+    if unroll > UNROLL:
+        trips = needed // unroll
+        lax.fori_loop(0, trips, stages(start, unroll), 0)
+        done = trips * unroll
+    trips = (needed - done + UNROLL - 1) // UNROLL
+    lax.fori_loop(0, trips, stages(start + done, UNROLL), 0)
 
 
 def scratch_of(rows, acc_blocks):
@@ -373,7 +383,16 @@
         ],
     )
     pair_loop(
-        lookup, 0, far, feat_f, feat_g, acc, rows // 8, 3 * (rows // 16), by_stage(scratch[4:])
+        lookup,
+        0,
+        far,
+        feat_f,
+        feat_g,
+        acc,
+        rows // 8,
+        3 * (rows // 16),
+        by_stage(scratch[4:]),
+        FAR_UNROLL,
     )
     for k, out in enumerate((o0, o1, o2)):
         for r in range(3):
@@ -403,13 +422,14 @@
                 out[pl.ds(r * tiles, tiles), :] += compact(acc, k, r, rows)
 
 
-def call(function, ins, out_shape, scratch, smem_in=1):
+def call(function, ins, out_shape, scratch, smem_in=1, any_in=0):
     smem = pl.BlockSpec(memory_space=pltpu.SMEM)
     vmem = pl.BlockSpec(memory_space=pltpu.VMEM)
+    anywhere = pl.BlockSpec(memory_space=pltpu.HBM)
     return pl.pallas_call(
         function,
         out_shape=out_shape,
-        in_specs=[smem if k < smem_in else vmem for k in range(len(ins))],
+        in_specs=[smem] * smem_in + [anywhere] * any_in + [vmem] * (len(ins) - smem_in - any_in),
         out_specs=[vmem] * len(out_shape),
         scratch_shapes=scratch,
         compiler_params=pltpu.CompilerParams(vmem_limit_bytes=40 * 2**20),

time: 66.6 us -> 65.9 us (0.989)
  Pallas kernels: 48.8 us -> 48 us
    pallas_call x4, Pallas kernels: 48.8 us -> 48 us  [call(): pl.pallas_call(function, out_shape=out_shape, in_specs=[smem] * smem_in +...]
where the time goes in v2:
time: 65.9 us; the launch traced here: 65.7 us
  Pallas kernels  48 us (73%)
  waiting for transfers between devices  8.81 us (13%)
  starting transfers between devices  5.55 us (8%)
  local copies, waits for them, and re-layouts  1.6 us (2%)
  other arithmetic  0.93 us (1%)
  between operations  0.79 us (1%)
    pallas_call x4, Pallas kernels, call(): pl.pallas_call(function, out_shape=out_shape, in_specs=[smem] * smem_in +...  48 us
    ppermute x4, waiting for transfers between devices, permute(): return lax.ppermute(x, AXES, pairs)  8.81 us
    ppermute x4, starting transfers between devices, permute(): return lax.ppermute(x, AXES, pairs)  5.55 us
  transfers between devices with their start and end apart: 4, of which 2 were waited for; matrix products, arithmetic and copies ran while one was open for 0% of the time, Pallas kernels for 19%

profile of v2, /device:TPU:2, one launch (start us, length us, event | category | flops | bytes accessed | tf_op | source)
XLA Modules:
  0.0 65.7 jit_solution(7075567985234043006)
XLA Ops:
  0.7 0.7 %fusion.1.code_ref = f32[1,128]{1,0:T(1,128)S(1)} fusion(s32[128]{0:T(128)} %param.9, s32[128]{0:T(128)} %param.10, s32[]{:T(128)S(6)} %add.36, s32[]{:T(128)} %bitcast.9), kind=kLoop, calls=%fused_computation.13 | loop fusion | flops 4992 | bytes 1544 | tf_op jit(solution)/shard_map/reshape | solution.py:457
  1.3 0.0 copy-start
  1.4 0.0 copy-start.1
  1.4 0.0 copy-start.2
  1.4 0.3 shard_map.64
  1.6 0.7 %copy-done = f32[3,16384]{1,0:T(4,128)S(1)} copy-done((f32[3,16384]{1,0:T(4,128)S(1)}, f32[3,16384]{1,0:T(4,128)}, u32[]{:S(2)}) %copy-start) | copy-done | bytes 196632
  2.3 0.1 copy-done.1
  2.4 0.0 copy-done.2
  2.4 0.2 maximum_bitcast_fusion
  2.7 0.1 collective-permute-start
  2.7 3.5 %collective-permute-start.1 = (f32[904,128]{1,0:T(8,128)S(1)}, f32[904,128]{1,0:T(8,128)S(1)}, u32[]{:S(2)}, u32[]{:S(2)}) collective-permute-start(f32[904,128]{1,0:T(8,128)S(1)} %pad_maximum_fusion.own), channel_id=1, source_target_pairs={{0,2},{1,3},{2,4},{3,5},{4,6},{5,7},{6,8},{7,9},{8,10},{9,11},{10,... | collective-permute-start | bytes 1388552 | tf_op jit(solution)/shard_map/ppermute | solution.py:471
  6.2 0.0 collective-permute-done.partner
  6.2 12.5 %shard_map.65 = (f32[384,128]{1,0:T(8,128)S(1)}, f32[384,128]{1,0:T(8,128)S(1)}, f32[6144,128]{1,0:T(8,128)S(1)}, f32[4096,128]{1,0:T(8,128)S(1)}) custom-call(s32[1]{0:T(128)} %bitcast.odd.odd_ref, f32[904,128]{1,0:T(8,128)S(1)} %pad_maximum_fusion.own, f32[904,128]{1,0:T(8,128)S(1)} %collective-permute-done.partner), custom_call_target="tpu_custom_call" | custom-call | flops 30000001024 | bytes 4000000 | tf_op jit(solution)/shard_map/pallas_call | solution.py:429
  18.8 1.6 %collective-permute-done.1.back = f32[904,128]{1,0:T(8,128)S(1)} collective-permute-done((f32[904,128]{1,0:T(8,128)S(1)}, f32[904,128]{1,0:T(8,128)S(1)}, u32[]{:S(2)}, u32[]{:S(2)}) %collective-permute-start.1) | collective-permute-done | bytes 462880 | tf_op jit(solution)/shard_map/ppermute | solution.py:471
  20.3 17.9 %shard_map.66 = (f32[384,128]{1,0:T(8,128)S(1)}, f32[384,128]{1,0:T(8,128)S(1)}, f32[384,128]{1,0:T(8,128)S(1)}) custom-call(s32[1]{0:T(128)} %bitcast.odd.odd_ref, f32[904,128]{1,0:T(8,128)S(1)} %pad_maximum_fusion.own, f32[904,128]{1,0:T(8,128)S(1)} %collective-permute-done.partner, f32[904,128]{1,0:T(8,128)S(1)} %collective-permute-done.1.back, ...), custom_call_target="tpu_custom_call" | custom-call | flops 30000001024 | bytes 4000000 | tf_op jit(solution)/shard_map/pallas_call | solution.py:429
  38.2 17.3 %shard_map.67 = (f32[384,128]{1,0:T(8,128)S(1)}, f32[384,128]{1,0:T(8,128)S(1)}) custom-call(s32[1]{0:T(128)} %bitcast.odd.odd_ref, f32[904,128]{1,0:T(8,128)S(1)} %pad_maximum_fusion.own, f32[904,128]{1,0:T(8,128)S(1)} %collective-permute-done.partner, f32[6144,128]{1,0:T(8,128)S(1)} %get-tuple-element.14.feat_f, f32[4096,128]{1,0:T(8,128)S(1)} %get-tuple-element.15.feat_g, ...), custom_call_target="tpu_custom_call" | custom-call | flops 30000001024 | bytes 4000000 | tf_op jit(solution)/shard_map/pallas_call | solution.py:429
  55.6 0.1 collective-permute-start.2
  55.6 1.9 %collective-permute-start.3 = (f32[384,128]{1,0:T(8,128)S(1)}, f32[384,128]{1,0:T(8,128)S(1)}, u32[]{:S(2)}, u32[]{:S(2)}) collective-permute-start(f32[384,128]{1,0:T(8,128)S(1)} %get-tuple-element.22), channel_id=1, source_target_pairs={{2,0},{3,1},{4,2},{5,3},{6,4},{7,5},{8,6},{9,7},{10,8},{11,9},{12,... | collective-permute-start | bytes 589832 | tf_op jit(solution)/shard_map/ppermute | solution.py:471
  57.6 0.0 collective-permute-done.2
  57.6 7.2 %collective-permute-done.3 = f32[384,128]{1,0:T(8,128)S(1)} collective-permute-done((f32[384,128]{1,0:T(8,128)S(1)}, f32[384,128]{1,0:T(8,128)S(1)}, u32[]{:S(2)}, u32[]{:S(2)}) %collective-permute-start.3) | collective-permute-done | bytes 196640 | tf_op jit(solution)/shard_map/ppermute | solution.py:471
  64.9 0.8 %reshape.20 = f32[3,16384]{1,0:T(4,128)} reshape(f32[384,128]{1,0:T(8,128)S(1)} %add_add_fusion) | data formatting | bytes 393216 | tf_op jit(solution)/shard_map/reshape | solution.py:502
  (3 shorter events, 0.1 us)
Async XLA Ops:
  1.3 1.0 %copy-start = (f32[3,16384]{1,0:T(4,128)S(1)}, f32[3,16384]{1,0:T(4,128)}, u32[]{:S(2)}) copy-start(f32[3,16384]{1,0:T(4,128)} %param.7) | copy-start | bytes 589828
  1.4 1.0 %copy-start.1 = (f32[3,16384]{1,0:T(4,128)S(1)}, f32[3,16384]{1,0:T(4,128)}, u32[]{:S(2)}) copy-start(f32[3,16384]{1,0:T(4,128)} %param.6) | copy-start | bytes 589828
  1.4 1.0 %copy-start.2 = (f32[16384]{0:T(1024)S(1)}, f32[16384]{0:T(1024)}, u32[]{:S(2)}) copy-start(f32[16384]{0:T(1024)} %param.8) | copy-start | bytes 196612
  2.7 3.6 %collective-permute-start = (f32[904,128]{1,0:T(8,128)S(1)}, f32[904,128]{1,0:T(8,128)S(1)}, u32[]{:S(2)}, u32[]{:S(2)}) collective-permute-start(f32[904,128]{1,0:T(8,128)S(1)} %pad_maximum_fusion.own), channel_id=1, source_target_pairs={{0,1},{1,0},{2,3},{3,2},{4,5},{5,4},{6,7},{7,6},{8,9},{9,8},{10,11... | collective-permute-start | bytes 1388552 | tf_op jit(solution)/shard_map/ppermute | solution.py:471
  2.7 17.6 %collective-permute-start.1 = (f32[904,128]{1,0:T(8,128)S(1)}, f32[904,128]{1,0:T(8,128)S(1)}, u32[]{:S(2)}, u32[]{:S(2)}) collective-permute-start(f32[904,128]{1,0:T(8,128)S(1)} %pad_maximum_fusion.own), channel_id=1, source_target_pairs={{0,2},{1,3},{2,4},{3,5},{4,6},{5,7},{6,8},{7,9},{8,10},{9,11},{10,... | collective-permute-start | bytes 1388552 | tf_op jit(solution)/shard_map/ppermute | solution.py:471
  55.6 2.0 %collective-permute-start.2 = (f32[384,128]{1,0:T(8,128)S(1)}, f32[384,128]{1,0:T(8,128)S(1)}, u32[]{:S(2)}, u32[]{:S(2)}) collective-permute-start(f32[384,128]{1,0:T(8,128)S(1)} %get-tuple-element.21), channel_id=1, source_target_pairs={{0,1},{1,0},{2,3},{3,2},{4,5},{5,4},{6,7},{7,6},{8,9},{9,8},{10,11... | collective-permute-start | bytes 589832 | tf_op jit(solution)/shard_map/ppermute | solution.py:471
  55.6 9.2 %collective-permute-start.3 = (f32[384,128]{1,0:T(8,128)S(1)}, f32[384,128]{1,0:T(8,128)S(1)}, u32[]{:S(2)}, u32[]{:S(2)}) collective-permute-start(f32[384,128]{1,0:T(8,128)S(1)} %get-tuple-element.22), channel_id=1, source_target_pairs={{2,0},{3,1},{4,2},{5,3},{6,4},{7,5},{8,6},{9,7},{10,8},{11,9},{12,... | collective-permute-start | bytes 589832 | tf_op jit(solution)/shard_map/ppermute | solution.py:471

commit v3 on v2

--- a/solution.py
+++ b/solution.py
@@ -10,11 +10,11 @@
 
 C = 256
 AXES = ("gx", "gy")
-UNROLL = 4
-FAR_UNROLL = 12
+UNROLL = 12
+TAIL = 4
 ROWS = 32
 TABLE = 8
-HEAD = 28
+HEAD = 34
 BALANCE = 13
 F32 = jnp.float32
 BF16 = jnp.bfloat16
@@ -59,7 +59,7 @@
     lax.fori_loop(0, (block.shape[0] - TABLE) // 56, step, 0)
 
 
-def pair_loop(lookup, start, stop, feat_f, feat_g, acc, b_shift, dummy, scratch, unroll=UNROLL):
+def pair_loop(lookup, start, stop, feat_f, feat_g, acc, b_shift, dummy, scratch):
     forms, terms, weights, row_part, col_part = scratch
 
     def clusters(t):
@@ -218,13 +218,11 @@
         return body
 
     needed = jnp.where(stop > start, stop - start + 2, 0)
-    done = 0
-    if unroll > UNROLL:
-        trips = needed // unroll
-        lax.fori_loop(0, trips, stages(start, unroll), 0)
-        done = trips * unroll
-    trips = (needed - done + UNROLL - 1) // UNROLL
-    lax.fori_loop(0, trips, stages(start + done, UNROLL), 0)
+    trips = needed // UNROLL
+    lax.fori_loop(0, trips, stages(start, UNROLL), 0)
+    done = trips * UNROLL
+    trips = (needed - done + TAIL - 1) // TAIL
+    lax.fori_loop(0, trips, stages(start + done, TAIL), 0)
 
 
 def scratch_of(rows, acc_blocks):
@@ -392,7 +390,6 @@
         rows // 8,
         3 * (rows // 16),
         by_stage(scratch[4:]),
-        FAR_UNROLL,
     )
     for k, out in enumerate((o0, o1, o2)):
         for r in range(3):

time: 65.9 us -> 62.7 us (0.951)
  Pallas kernels: 48 us -> 45.6 us
  waiting for transfers between devices: 8.81 us -> 8.02 us
    pallas_call x4, Pallas kernels: 48 us -> 45.6 us  [call(): pl.pallas_call(function, out_shape=out_shape, in_specs=[smem] * smem_in +...]
    ppermute x4, waiting for transfers between devices: 8.81 us -> 8.02 us  [permute(): return lax.ppermute(x, AXES, pairs)]
  transfers between devices with their start and end apart: 4 -> 4, of which waited for: 2 -> 2; matrix products, arithmetic and copies ran while one was open for 0% -> 0% of each run, Pallas kernels for 19% -> 21%
where the time goes in v3:
time: 62.7 us; the launch traced here: 62.5 us
  Pallas kernels  45.6 us (73%)
  waiting for transfers between devices  8.02 us (13%)
  starting transfers between devices  5.55 us (9%)
  local copies, waits for them, and re-layouts  1.6 us (3%)
  other arithmetic  0.93 us (1%)
  between operations  0.79 us (1%)
    pallas_call x4, Pallas kernels, call(): pl.pallas_call(function, out_shape=out_shape, in_specs=[smem] * smem_in +...  45.6 us
    ppermute x4, waiting for transfers between devices, permute(): return lax.ppermute(x, AXES, pairs)  8.02 us
    ppermute x4, starting transfers between devices, permute(): return lax.ppermute(x, AXES, pairs)  5.55 us
  transfers between devices with their start and end apart: 4, of which 2 were waited for; matrix products, arithmetic and copies ran while one was open for 0% of the time, Pallas kernels for 21%

profile of v3, /device:TPU:2, one launch (start us, length us, event | category | flops | bytes accessed | tf_op | source)
XLA Modules:
  0.0 62.5 jit_solution(16282081169541250805)
XLA Ops:
  0.7 0.7 %fusion.1.code_ref = f32[1,128]{1,0:T(1,128)S(1)} fusion(s32[128]{0:T(128)} %param.9, s32[128]{0:T(128)} %param.10, s32[]{:T(128)S(6)} %add.36, s32[]{:T(128)} %bitcast.9), kind=kLoop, calls=%fused_computation.13 | loop fusion | flops 4992 | bytes 1544 | tf_op jit(solution)/shard_map/reshape | solution.py:454
  1.3 0.0 copy-start
  1.4 0.0 copy-start.1
  1.4 0.0 copy-start.2
  1.4 0.3 shard_map.64
  1.6 0.7 %copy-done = f32[3,16384]{1,0:T(4,128)S(1)} copy-done((f32[3,16384]{1,0:T(4,128)S(1)}, f32[3,16384]{1,0:T(4,128)}, u32[]{:S(2)}) %copy-start) | copy-done | bytes 196632
  2.3 0.1 copy-done.1
  2.4 0.0 copy-done.2
  2.4 0.2 maximum_bitcast_fusion
  2.7 0.1 collective-permute-start
  2.7 3.5 %collective-permute-start.1 = (f32[904,128]{1,0:T(8,128)S(1)}, f32[904,128]{1,0:T(8,128)S(1)}, u32[]{:S(2)}, u32[]{:S(2)}) collective-permute-start(f32[904,128]{1,0:T(8,128)S(1)} %pad_maximum_fusion.own), channel_id=1, source_target_pairs={{0,2},{1,3},{2,4},{3,5},{4,6},{5,7},{6,8},{7,9},{8,10},{9,11},{10,... | collective-permute-start | bytes 1388552 | tf_op jit(solution)/shard_map/ppermute | solution.py:468
  6.2 0.0 collective-permute-done.partner
  6.2 13.3 %shard_map.65 = (f32[384,128]{1,0:T(8,128)S(1)}, f32[384,128]{1,0:T(8,128)S(1)}, f32[6144,128]{1,0:T(8,128)S(1)}, f32[4096,128]{1,0:T(8,128)S(1)}) custom-call(s32[1]{0:T(128)} %bitcast.odd.odd_ref, f32[904,128]{1,0:T(8,128)S(1)} %pad_maximum_fusion.own, f32[904,128]{1,0:T(8,128)S(1)} %collective-permute-done.partner), custom_call_target="tpu_custom_call" | custom-call | flops 30000001024 | bytes 4000000 | tf_op jit(solution)/shard_map/pallas_call | solution.py:426
  19.6 0.8 %collective-permute-done.1.back = f32[904,128]{1,0:T(8,128)S(1)} collective-permute-done((f32[904,128]{1,0:T(8,128)S(1)}, f32[904,128]{1,0:T(8,128)S(1)}, u32[]{:S(2)}, u32[]{:S(2)}) %collective-permute-start.1) | collective-permute-done | bytes 462880 | tf_op jit(solution)/shard_map/ppermute | solution.py:468
  20.3 18.1 %shard_map.66 = (f32[384,128]{1,0:T(8,128)S(1)}, f32[384,128]{1,0:T(8,128)S(1)}, f32[384,128]{1,0:T(8,128)S(1)}) custom-call(s32[1]{0:T(128)} %bitcast.odd.odd_ref, f32[904,128]{1,0:T(8,128)S(1)} %pad_maximum_fusion.own, f32[904,128]{1,0:T(8,128)S(1)} %collective-permute-done.partner, f32[904,128]{1,0:T(8,128)S(1)} %collective-permute-done.1.back, ...), custom_call_target="tpu_custom_call" | custom-call | flops 30000001024 | bytes 4000000 | tf_op jit(solution)/shard_map/pallas_call | solution.py:426
  38.4 14.0 %shard_map.67 = (f32[384,128]{1,0:T(8,128)S(1)}, f32[384,128]{1,0:T(8,128)S(1)}) custom-call(s32[1]{0:T(128)} %bitcast.odd.odd_ref, f32[904,128]{1,0:T(8,128)S(1)} %pad_maximum_fusion.own, f32[904,128]{1,0:T(8,128)S(1)} %collective-permute-done.partner, f32[6144,128]{1,0:T(8,128)S(1)} %get-tuple-element.14.feat_f, f32[4096,128]{1,0:T(8,128)S(1)} %get-tuple-element.15.feat_g, ...), custom_call_target="tpu_custom_call" | custom-call | flops 30000001024 | bytes 4000000 | tf_op jit(solution)/shard_map/pallas_call | solution.py:426
  52.4 0.1 collective-permute-start.2
  52.5 1.9 %collective-permute-start.3 = (f32[384,128]{1,0:T(8,128)S(1)}, f32[384,128]{1,0:T(8,128)S(1)}, u32[]{:S(2)}, u32[]{:S(2)}) collective-permute-start(f32[384,128]{1,0:T(8,128)S(1)} %get-tuple-element.22), channel_id=1, source_target_pairs={{2,0},{3,1},{4,2},{5,3},{6,4},{7,5},{8,6},{9,7},{10,8},{11,9},{12,... | collective-permute-start | bytes 589832 | tf_op jit(solution)/shard_map/ppermute | solution.py:468
  54.4 0.0 collective-permute-done.2
  54.4 7.2 %collective-permute-done.3 = f32[384,128]{1,0:T(8,128)S(1)} collective-permute-done((f32[384,128]{1,0:T(8,128)S(1)}, f32[384,128]{1,0:T(8,128)S(1)}, u32[]{:S(2)}, u32[]{:S(2)}) %collective-permute-start.3) | collective-permute-done | bytes 196640 | tf_op jit(solution)/shard_map/ppermute | solution.py:468
  61.7 0.8 %reshape.20 = f32[3,16384]{1,0:T(4,128)} reshape(f32[384,128]{1,0:T(8,128)S(1)} %add_add_fusion) | data formatting | bytes 393216 | tf_op jit(solution)/shard_map/reshape | solution.py:499
  (3 shorter events, 0.1 us)
Async XLA Ops:
  1.3 1.0 %copy-start = (f32[3,16384]{1,0:T(4,128)S(1)}, f32[3,16384]{1,0:T(4,128)}, u32[]{:S(2)}) copy-start(f32[3,16384]{1,0:T(4,128)} %param.7) | copy-start | bytes 589828
  1.4 1.0 %copy-start.1 = (f32[3,16384]{1,0:T(4,128)S(1)}, f32[3,16384]{1,0:T(4,128)}, u32[]{:S(2)}) copy-start(f32[3,16384]{1,0:T(4,128)} %param.6) | copy-start | bytes 589828
  1.4 1.0 %copy-start.2 = (f32[16384]{0:T(1024)S(1)}, f32[16384]{0:T(1024)}, u32[]{:S(2)}) copy-start(f32[16384]{0:T(1024)} %param.8) | copy-start | bytes 196612
  2.7 3.6 %collective-permute-start = (f32[904,128]{1,0:T(8,128)S(1)}, f32[904,128]{1,0:T(8,128)S(1)}, u32[]{:S(2)}, u32[]{:S(2)}) collective-permute-start(f32[904,128]{1,0:T(8,128)S(1)} %pad_maximum_fusion.own), channel_id=1, source_target_pairs={{0,1},{1,0},{2,3},{3,2},{4,5},{5,4},{6,7},{7,6},{8,9},{9,8},{10,11... | collective-permute-start | bytes 1388552 | tf_op jit(solution)/shard_map/ppermute | solution.py:468
  2.7 17.6 %collective-permute-start.1 = (f32[904,128]{1,0:T(8,128)S(1)}, f32[904,128]{1,0:T(8,128)S(1)}, u32[]{:S(2)}, u32[]{:S(2)}) collective-permute-start(f32[904,128]{1,0:T(8,128)S(1)} %pad_maximum_fusion.own), channel_id=1, source_target_pairs={{0,2},{1,3},{2,4},{3,5},{4,6},{5,7},{6,8},{7,9},{8,10},{9,11},{10,... | collective-permute-start | bytes 1388552 | tf_op jit(solution)/shard_map/ppermute | solution.py:468
  52.4 2.0 %collective-permute-start.2 = (f32[384,128]{1,0:T(8,128)S(1)}, f32[384,128]{1,0:T(8,128)S(1)}, u32[]{:S(2)}, u32[]{:S(2)}) collective-permute-start(f32[384,128]{1,0:T(8,128)S(1)} %get-tuple-element.21), channel_id=1, source_target_pairs={{0,1},{1,0},{2,3},{3,2},{4,5},{5,4},{6,7},{7,6},{8,9},{9,8},{10,11... | collective-permute-start | bytes 589832 | tf_op jit(solution)/shard_map/ppermute | solution.py:468
  52.5 9.2 %collective-permute-start.3 = (f32[384,128]{1,0:T(8,128)S(1)}, f32[384,128]{1,0:T(8,128)S(1)}, u32[]{:S(2)}, u32[]{:S(2)}) collective-permute-start(f32[384,128]{1,0:T(8,128)S(1)} %get-tuple-element.22), channel_id=1, source_target_pairs={{2,0},{3,1},{4,2},{5,3},{6,4},{7,5},{8,6},{9,7},{10,8},{11,9},{12,... | collective-permute-start | bytes 589832 | tf_op jit(solution)/shard_map/ppermute | solution.py:468
